TPU v7x, 32 devices: a whole 2x2x4 slice. The times are simulated.
32 devices in a mesh: groups: 2 (over y), fibre: 4 (over z), seg: 2 (over x), rec: 2 (over core).
Axes of the slice: x: 2, y: 2, z: 4, core: 2. Of those that a mesh axis runs over, the one named last changes fastest.
Arguments:
- records: bfloat16 [2, 2048, 1024], P('rec', 'fibre', ('groups', 'seg')), parts along dimension 2, may hold values from -6 to 6
- pairs: int32 [16, 2], replicated, may hold values from 0 to 15
- observed: float32 [32, 32, 256], P(('groups', 'fibre', 'seg')), parts along dimension 0, may hold values from -6 to 6
- lag_mask: int32 [32, 256], P(('groups', 'fibre', 'seg')), parts along dimension 0, may hold values 0 or 1
Outputs:
- adjoint_sources: bfloat16 [2, 2048, 1024], P('rec', 'fibre', ('groups', 'seg')), parts along dimension 2
There are 2 independent parts, one for each index of `groups`. A program takes and returns all parts, laid end to end along the dimension named above; an argument that names none is the same for every part. Nothing has to cross between parts.
All inputs are finite; a program needn't handle non-finite values. No bound on the sum of `lag_mask` on one device may be relied on, other than what follows from the above.
Results may differ from a plain program's by a relative error of at most 0.015.
Values may be sent and summed in bfloat16 or wider, within the bound.
A program may use at most 64 MiB of HBM per device.

v0:
```python
import jax
import jax.numpy as jnp
from jax import lax
from jax.sharding import PartitionSpec as P

S = 2048
F = 1024
LAGS = 256
BLOCK = 32
CH_DEV = 64


def forward_table():
    freq_index = jnp.arange(F, dtype=jnp.int32)
    time_index = jnp.arange(S, dtype=jnp.int32)
    phase = freq_index[:, None] * time_index[None, :] % S
    angles = phase.astype(jnp.float32) * (2.0 * jnp.pi / S)
    scale = 1.0 / jnp.sqrt(jnp.float32(S))
    return jnp.stack(
        [
            (jnp.cos(angles) * scale).astype(jnp.bfloat16),
            (-jnp.sin(angles) * scale).astype(jnp.bfloat16),
        ],
        axis=1,
    )


def lag_table():
    freq_index = jnp.arange(F, dtype=jnp.int32)
    shifts = (jnp.arange(LAGS, dtype=jnp.int32) - LAGS // 2) % S
    phase = freq_index[:, None] * shifts[None, :] % S
    angles = phase.astype(jnp.float32) * (2.0 * jnp.pi / S)
    scale = 1.0 / jnp.sqrt(jnp.float32(F))
    return jnp.stack(
        [
            (jnp.cos(angles) * scale).astype(jnp.bfloat16),
            (-jnp.sin(angles) * scale).astype(jnp.bfloat16),
        ],
        axis=1,
    )


def synthesize(incoming, table):
    count = incoming.shape[-1]
    flat = incoming.reshape(2 * F, count)
    result = jnp.einsum(
        "qn,qt->tn", flat, table.reshape(2 * F, S), preferred_element_type=jnp.float32
    )
    return result.astype(jnp.bfloat16)


def on_device(records, pairs, observed, lag_mask):
    fibre_count = lax.axis_size("fibre")
    seg_count = lax.axis_size("seg")
    spread_count = fibre_count * seg_count
    freq_dev = F // spread_count
    blocks_dev = CH_DEV // BLOCK
    block_count = CH_DEV * spread_count // BLOCK
    pair_total = pairs.shape[0]
    pairs_dev = pair_total // spread_count
    table = forward_table()
    lags = lag_table()
    spans = records.reshape(1, S // fibre_count, fibre_count, CH_DEV)
    incoming = lax.all_to_all(spans, "fibre", split_axis=2, concat_axis=1, tiled=True)
    count = incoming.shape[3]
    signal = incoming.reshape(S, count)
    result = jnp.einsum(
        "qs,sn->qn", table.reshape(2 * F, S), signal, preferred_element_type=jnp.float32
    )
    spectra = result.reshape(F, 2, count).astype(jnp.bfloat16)
    widened = lax.all_to_all(spectra, ("fibre", "seg"), split_axis=0, concat_axis=2, tiled=True)
    seg_blocks = fibre_count * blocks_dev
    slot_ids = (
        pairs % seg_blocks // blocks_dev * seg_count + pairs // seg_blocks
    ) * blocks_dev + pairs % blocks_dev
    blocks_grid = widened.reshape(freq_dev, 2, block_count, BLOCK)
    first_side = jnp.take(blocks_grid, slot_ids[:, 0], axis=2).astype(jnp.float32)
    second_side = jnp.take(blocks_grid, slot_ids[:, 1], axis=2).astype(jnp.float32)
    first_re, first_im = (first_side[:, 0], first_side[:, 1])
    second_re, second_im = (second_side[:, 0], second_side[:, 1])
    cross_re = first_re * second_re + first_im * second_im
    cross_im = first_im * second_re - first_re * second_im
    cross_spec = jnp.stack([cross_re, cross_im], axis=1).astype(jnp.bfloat16)
    cross_spec = cross_spec.reshape(freq_dev, 2, spread_count, pairs_dev * BLOCK)
    owned_spec = lax.all_to_all(
        cross_spec, ("fibre", "seg"), split_axis=2, concat_axis=0, tiled=True
    )
    owned_spec = owned_spec.reshape(F, 2, pairs_dev * BLOCK)
    partial_corr = jnp.einsum("wpx,wpl->xl", owned_spec, lags, preferred_element_type=jnp.float32)
    synthetic = (
        lax.psum(partial_corr.astype(jnp.bfloat16), "rec")
        .astype(jnp.float32)
        .reshape(pairs_dev, BLOCK, LAGS)
    )
    weights = lag_mask[:, None, :].astype(jnp.float32) * jnp.tanh(synthetic - observed)
    weights_low = weights.astype(jnp.bfloat16).reshape(pairs_dev * BLOCK, LAGS)
    adjoint_spec = jnp.einsum("xl,wpl->wpx", weights_low, lags, preferred_element_type=jnp.float32)
    adjoint_spec = adjoint_spec.astype(jnp.bfloat16).reshape(F, 2, 1, pairs_dev * BLOCK)
    returned = lax.all_to_all(
        adjoint_spec, ("fibre", "seg"), split_axis=0, concat_axis=2, tiled=True
    )
    returned = returned.reshape(freq_dev, 2, pair_total, BLOCK).astype(jnp.float32)
    adjoint_re, adjoint_im = (returned[:, 0], returned[:, 1])
    grad_first = jnp.stack(
        [
            adjoint_re * second_re - adjoint_im * second_im,
            adjoint_re * second_im + adjoint_im * second_re,
        ],
        axis=1,
    )
    grad_second = jnp.stack(
        [
            adjoint_re * first_re + adjoint_im * first_im,
            adjoint_re * first_im - adjoint_im * first_re,
        ],
        axis=1,
    )
    contributions = jnp.concatenate([grad_first, grad_second], axis=2)
    endpoint_ids = jnp.concatenate([slot_ids[:, 0], slot_ids[:, 1]])
    summed = jax.ops.segment_sum(
        jnp.moveaxis(contributions, 2, 0), endpoint_ids, num_segments=block_count
    )
    block_adjoint = jnp.moveaxis(summed, 0, 2).astype(jnp.bfloat16)
    outgoing = block_adjoint.reshape(freq_dev, 2, spread_count, CH_DEV)
    sources = synthesize(
        lax.all_to_all(outgoing, ("fibre", "seg"), split_axis=2, concat_axis=0, tiled=True), table
    )
    regrouped = lax.all_to_all(sources, "fibre", split_axis=0, concat_axis=1, tiled=True)
    return regrouped[None]


def solution(mesh):
    in_specs = (
        P("rec", "fibre", ("groups", "seg")),
        P(),
        P(("groups", "fibre", "seg"), None, None),
        P(("groups", "fibre", "seg"), None),
    )
    out_specs = P("rec", "fibre", ("groups", "seg"))
    return jax.shard_map(
        on_device, mesh=mesh, in_specs=in_specs, out_specs=out_specs, check_vma=False
    )
```

profile of v0, /device:TPU:0, one launch (start us, length us, event | category | flops | bytes accessed | tf_op | source)
XLA Modules:
  0.0 163.2 jit_solution(8597783628842389983)
XLA Ops:
  0.0 1.8 %copy.59 = bf16[1,512,256]{1,2,0:T(8,128)(2,1)} copy(bf16[1,512,256]{2,1,0:T(8,128)(2,1)} %param.6) | data formatting | bytes 524288 | tf_op args[0]
  1.8 6.3 %all-to-all-start = ((bf16[1,512,4,64]{1,3,0,2:T(8,128)(2,1)}), bf16[1,512,4,64]{1,3,0,2:T(8,128)(2,1)S(1)}, u32[]{:S(2)}, u32[]{:S(2)}) async-start(bf16[1,512,4,64]{1,3,0,2:T(8,128)(2,1)} %bitcast.3), calls=%async_computation | async-start | bytes 524288 | tf_op jit(solution)/shard_map/all_to_all | solution.py:64
  8.1 35.0 %multiply_convert_fusion = (bf16[1024,1,2048]{2,0,1:T(8,128)(2,1)}, bf16[1024,1,2048]{2,0,1:T(8,128)(2,1)}) fusion(), kind=kLoop, calls=%fused_computation.10 | loop fusion | flops 39845888 | bytes 8388608 | tf_op jit(solution)/shard_map/convert_element_type | solution.py:22
  43.2 0.2 copy.61
  43.4 0.2 reshape.311
  43.6 5.1 %convolution_convert_fusion.1 = bf16[1024,2,64]{0,2,1:T(8,128)(2,1)S(1)} fusion(bf16[2048,64,1]{0,1,2:T(8,128)(2,1)S(1)} %reshape.311, bf16[1024,1,2048]{2,0,1:T(8,128)(2,1)} %get-tuple-element.24, bf16[1024,1,2048]{2,0,1:T(8,128)(2,1)} %get-tuple-element.25), kind=kOutput, calls=%fused_computation.19 | convolution fusion | flops 541196288 | bytes 8912896 | tf_op jit(solution)/shard_map/qs,sn->qn/dot_general | solution.py:67
  48.7 0.4 copy.62
  49.1 1.1 reshape.316
  50.2 6.0 %all-to-all-start.1 = ((bf16[8,2,8192]{2,1,0:T(2,128)(2,1)}), bf16[8,2,8192]{2,1,0:T(2,128)(2,1)S(1)}, u32[]{:S(2)}, u32[]{:S(2)}) async-start(bf16[8,2,8192]{2,1,0:T(2,128)(2,1)} %reshape.316), calls=%async_computation.1 | async-start | bytes 524288 | tf_op jit(solution)/shard_map/all_to_all | solution.py:71
  56.3 8.4 %all-to-all-done.1 = bf16[8,2,8192]{2,1,0:T(2,128)(2,1)S(1)} async-done(((bf16[8,2,8192]{2,1,0:T(2,128)(2,1)}), bf16[8,2,8192]{2,1,0:T(2,128)(2,1)S(1)}, u32[]{:S(2)}, u32[]{:S(2)}) %all-to-all-start.1) | async-done | bytes 262176 | tf_op jit(solution)/shard_map/all_to_all | solution.py:71
  64.7 0.3 reshape.317
  65.1 0.4 copy.79
  65.5 0.6 gather_fusion.1
  66.1 0.6 gather_fusion
  66.7 0.1 bitcast_convert_fusion
  66.8 0.1 bitcast_convert_fusion.1
  66.9 0.1 add_convert_fusion
  67.0 0.7 pad_maximum_fusion.4
  67.8 3.4 %all-to-all-start.2 = ((bf16[128,2,8,64]{0,3,1,2:T(8,128)(2,1)}), bf16[128,2,8,64]{0,3,1,2:T(8,128)(2,1)S(1)}, u32[]{:S(2)}, u32[]{:S(2)}) async-start(bf16[128,2,8,64]{0,3,1,2:T(8,128)(2,1)} %pad_maximum_fusion.4), calls=%async_computation.2 | async-start | bytes 524288 | tf_op jit(solution)/shard_map/all_to_all | solution.py:85
  71.2 4.5 %multiply_convert_fusion.3 = (bf16[1024,1,256]{2,0,1:T(8,128)(2,1)S(1)}, bf16[1024,1,256]{2,0,1:T(8,128)(2,1)S(1)}) fusion(s32[256]{0:T(256)S(1)} %and_select_fusion), kind=kLoop, calls=%fused_computation.30 | loop fusion | flops 4980736 | bytes 1049600 | tf_op jit(solution)/shard_map/convert_element_type | solution.py:36
  75.7 4.0 %all-to-all-done.2 = bf16[128,2,8,64]{0,3,1,2:T(8,128)(2,1)S(1)} async-done(((bf16[128,2,8,64]{0,3,1,2:T(8,128)(2,1)}), bf16[128,2,8,64]{0,3,1,2:T(8,128)(2,1)S(1)}, u32[]{:S(2)}, u32[]{:S(2)}) %all-to-all-start.2) | async-done | bytes 262176 | tf_op jit(solution)/shard_map/all_to_all | solution.py:85
  79.7 0.2 copy.67
  79.9 0.1 reshape.271
  80.0 0.3 fusion.7
  80.3 3.4 %psum.7 = bf16[2,32,256]{2,1,0:T(8,128)(2,1)S(1)} all-reduce(bf16[2,32,256]{2,1,0:T(8,128)(2,1)S(1)} %bitcast.121), channel_id=1, replica_groups=mesh['groups'=2,'fibre'=4,'seg'=2,'rec'=2] {'rec'}, use_global_device_ids=true, to_apply=%region_0.2 | all-reduce | flops 16384 | bytes 65536 | tf_op jit(solution)/shard_map/psum | solution.py:91
  83.8 0.4 fusion.6
  84.2 0.4 copy.68
  84.6 1.1 reshape.318
  85.7 3.6 %all-to-all-start.3 = ((bf16[8,2,8192]{2,1,0:T(2,128)(2,1)}), bf16[8,2,8192]{2,1,0:T(2,128)(2,1)S(1)}, u32[]{:S(2)}, u32[]{:S(2)}) async-start(bf16[8,2,8192]{2,1,0:T(2,128)(2,1)} %reshape.318), calls=%async_computation.3 | async-start | bytes 524288 | tf_op jit(solution)/shard_map/all_to_all | solution.py:99
  89.3 0.1 pad_add_fusion
  89.3 9.4 %all-to-all-done.3 = bf16[8,2,8192]{2,1,0:T(2,128)(2,1)S(1)} async-done(((bf16[8,2,8192]{2,1,0:T(2,128)(2,1)}), bf16[8,2,8192]{2,1,0:T(2,128)(2,1)S(1)}, u32[]{:S(2)}, u32[]{:S(2)}) %all-to-all-start.3) | async-done | bytes 262176 | tf_op jit(solution)/shard_map/all_to_all | solution.py:99
  98.8 0.3 reshape.319
  99.1 0.4 copy.69
  99.6 0.1 copy.83
  99.7 0.1 copy.70
  99.8 0.2 multiply_subtract_fusion.1
  100.0 0.1 maximum_bitcast_fusion
  100.1 0.1 broadcast_in_dim.23
  100.1 2.1 %scatter_fusion = f32[16,128,2,32]{1,3,2,0:T(8,128)S(1)} fusion(f32[16,128,2,32]{1,3,2,0:T(8,128)S(1)} %broadcast_in_dim.23, s32[32]{0:T(128)S(1)} %pad_add_fusion, f32[32,128,2,32]{1,3,2,0:T(8,128)S(1)} %maximum_bitcast_fusion), kind=kCustom, calls=%fused_computation.2 | custom fusion | flops 262144 | bytes 3145856 | tf_op jit(solution)/shard_map/scatter-add | solution.py:120
  102.3 0.7 copy.74
  103.0 3.6 %all-to-all-start.4 = ((bf16[128,2,8,64]{0,3,1,2:T(8,128)(2,1)}), bf16[128,2,8,64]{0,3,1,2:T(8,128)(2,1)S(1)}, u32[]{:S(2)}, u32[]{:S(2)}) async-start(bf16[128,2,8,64]{0,3,1,2:T(8,128)(2,1)} %copy.74), calls=%async_computation.4 | async-start | bytes 524288 | tf_op jit(solution)/shard_map/all_to_all | solution.py:126
  106.6 7.5 %pad_maximum_fusion = bf16[1024,2,2048]{2,0,1:T(8,128)(2,1)} fusion(bf16[1024,1,2048]{2,0,1:T(8,128)(2,1)} %get-tuple-element.24, bf16[1024,1,2048]{2,0,1:T(8,128)(2,1)} %get-tuple-element.25), kind=kLoop, calls=%fused_computation.9 | loop fusion | flops 4194304 | bytes 16777216 | tf_op jit(solution)/shard_map/stack | solution.py:19
  114.1 16.4 %copy.58 = bf16[1024,2,2048]{2,1,0:T(2,128)(2,1)} copy(bf16[1024,2,2048]{2,0,1:T(8,128)(2,1)} %pad_maximum_fusion) | data formatting | bytes 16777216 | tf_op jit(solution)/shard_map/stack | solution.py:19
  130.5 13.1 %reshape.267 = bf16[2048,2048]{1,0:T(8,128)(2,1)} reshape(bf16[1024,2,2048]{2,1,0:T(2,128)(2,1)} %copy.58) | data formatting | bytes 16777216 | tf_op jit(solution)/shard_map/reshape | solution.py:47
  143.6 0.4 copy.75
  144.0 5.0 %convolution_convert_fusion = bf16[2048,64]{0,1:T(8,128)(2,1)S(1)} fusion(bf16[2048,2048]{1,0:T(8,128)(2,1)} %reshape.267, bf16[2048,64]{1,0:T(8,128)(2,1)S(1)} %bitcast.106), kind=kOutput, calls=%fused_computation.15 | convolution fusion | flops 537001984 | bytes 8912896 | tf_op jit(solution)/shard_map/qn,qt->tn/dot_general | solution.py:46
  149.1 13.3 %all_to_all.85 = bf16[4,512,64]{1,2,0:T(8,128)(2,1)S(1)} all-to-all(bf16[4,512,64]{1,2,0:T(8,128)(2,1)S(1)} %bitcast.117), channel_id=1, replica_groups=mesh['groups'=2,'fibre'=4,'seg'=2,'rec'=2] {'fibre'}, dimensions={0} | all-to-all | bytes 524288 | tf_op jit(solution)/shard_map/all_to_all | solution.py:128
  162.3 0.8 copy.77
  (19 shorter events, 0.2 us)
Async XLA Ops:
  1.8 41.4 %all-to-all-start = ((bf16[1,512,4,64]{1,3,0,2:T(8,128)(2,1)}), bf16[1,512,4,64]{1,3,0,2:T(8,128)(2,1)S(1)}, u32[]{:S(2)}, u32[]{:S(2)}) async-start(bf16[1,512,4,64]{1,3,0,2:T(8,128)(2,1)} %bitcast.3), calls=%async_computation | async-start | bytes 524288 | tf_op jit(solution)/shard_map/all_to_all | solution.py:64
  43.6 12.6 %copy-start.2 = (s32[16,2]{0,1:T(2,128)S(1)}, s32[16,2]{0,1:T(2,128)}, u32[]{:S(2)}) copy-start(s32[16,2]{0,1:T(2,128)} %param.7) | copy-start | bytes 388
  48.7 22.5 %copy-start.1 = (s32[2,256]{1,0:T(2,128)S(1)}, s32[2,256]{1,0:T(2,128)}, u32[]{:S(2)}) copy-start(s32[2,256]{1,0:T(2,128)} %param.9) | copy-start | bytes 6148
  48.7 35.0 %copy-start = (f32[2,32,256]{2,1,0:T(8,128)S(1)}, f32[2,32,256]{2,1,0:T(8,128)}, u32[]{:S(2)}) copy-start(f32[2,32,256]{2,1,0:T(8,128)} %param.8) | copy-start | bytes 196612
  50.2 14.5 %all-to-all-start.1 = ((bf16[8,2,8192]{2,1,0:T(2,128)(2,1)}), bf16[8,2,8192]{2,1,0:T(2,128)(2,1)S(1)}, u32[]{:S(2)}, u32[]{:S(2)}) async-start(bf16[8,2,8192]{2,1,0:T(2,128)(2,1)} %reshape.316), calls=%async_computation.1 | async-start | bytes 524288 | tf_op jit(solution)/shard_map/all_to_all | solution.py:71
  67.8 12.0 %all-to-all-start.2 = ((bf16[128,2,8,64]{0,3,1,2:T(8,128)(2,1)}), bf16[128,2,8,64]{0,3,1,2:T(8,128)(2,1)S(1)}, u32[]{:S(2)}, u32[]{:S(2)}) async-start(bf16[128,2,8,64]{0,3,1,2:T(8,128)(2,1)} %pad_maximum_fusion.4), calls=%async_computation.2 | async-start | bytes 524288 | tf_op jit(solution)/shard_map/all_to_all | solution.py:85
  85.7 13.1 %all-to-all-start.3 = ((bf16[8,2,8192]{2,1,0:T(2,128)(2,1)}), bf16[8,2,8192]{2,1,0:T(2,128)(2,1)S(1)}, u32[]{:S(2)}, u32[]{:S(2)}) async-start(bf16[8,2,8192]{2,1,0:T(2,128)(2,1)} %reshape.318), calls=%async_computation.3 | async-start | bytes 524288 | tf_op jit(solution)/shard_map/all_to_all | solution.py:99
  103.0 40.6 %all-to-all-start.4 = ((bf16[128,2,8,64]{0,3,1,2:T(8,128)(2,1)}), bf16[128,2,8,64]{0,3,1,2:T(8,128)(2,1)S(1)}, u32[]{:S(2)}, u32[]{:S(2)}) async-start(bf16[128,2,8,64]{0,3,1,2:T(8,128)(2,1)} %copy.74), calls=%async_computation.4 | async-start | bytes 524288 | tf_op jit(solution)/shard_map/all_to_all | solution.py:126
where the time goes:
time: 164 us; the launch traced here: 163 us
  other arithmetic  50.7 us (31%)
  local copies, waits for them, and re-layouts  39.9 us (24%)
  starting transfers between devices  23 us (14%)
  waiting for transfers between devices  21.9 us (13%)
  blocking collectives  16.7 us (10%)
  matrix products  10.8 us (7%)
    convert_element_type x1, other arithmetic, forward_table(): (-jnp.sin(angles) * scale).astype(jnp.bfloat16)  35 us
    another operation x1, local copies, waits for them, and re-layouts, forward_table(): jnp.stack([(jnp.cos(angles) * scale).astype(jnp.bfloat16), (-jnp.sin(angl...  16.4 us
    all_to_all x1, blocking collectives, on_device(): lax.all_to_all(sources, 'fibre', split_axis=0, concat_axis=1, tiled=True)  13.3 us
    reshape x1, local copies, waits for them, and re-layouts, synthesize(): table.reshape(2 * F, S)  13.1 us
    all_to_all x1, waiting for transfers between devices, on_device(): lax.all_to_all(adjoint_spec, ('fibre', 'seg'), split_axis=0, concat_axis=...  9.42 us
    all_to_all x1, waiting for transfers between devices, on_device(): lax.all_to_all(spectra, ('fibre', 'seg'), split_axis=0, concat_axis=2, ti...  8.44 us
    another operation x1, other arithmetic, forward_table(): jnp.stack([(jnp.cos(angles) * scale).astype(jnp.bfloat16), (-jnp.sin(angl...  7.45 us
    all_to_all x1, starting transfers between devices, on_device(): lax.all_to_all(spans, 'fibre', split_axis=2, concat_axis=1, tiled=True)  6.35 us
  transfers between devices with their start and end apart: 5, of which 3 were waited for; matrix products, arithmetic and copies ran while one was open for 47% of the time, Pallas kernels for 0%

commit v1 on v0

--- a/solution.py
+++ b/solution.py
@@ -1,6 +1,11 @@
+import functools
+
 import jax
 import jax.numpy as jnp
+import numpy as np
 from jax import lax
+from jax.experimental import pallas as pl
+from jax.experimental.pallas import tpu as pltpu
 from jax.sharding import PartitionSpec as P
 
 S = 2048
@@ -129,6 +134,280 @@
     return regrouped[None]
 
 
+def angle_parts(freqs, times, scale):
+    phase = (freqs[:, None].astype(np.int64) * times[None, :]) % S
+    angles = phase.astype(np.float32) * np.float32(2.0 * np.pi / S)
+    return np.stack([np.cos(angles) * scale, -np.sin(angles) * scale])
+
+
+def band_tables(spread_count):
+    order = np.concatenate([np.arange(0, F, 2), np.arange(1, F, 2)]).reshape(spread_count, -1)
+    half = np.arange(S // 2)
+    scale = np.float32(1.0) / np.sqrt(np.float32(S))
+    forward = np.concatenate(
+        [angle_parts(band, half, scale).reshape(-1, S // 2) for band in order]
+    )
+    backward = np.stack([forward[:F].T, forward[F:].T])
+    shifts = (np.arange(LAGS) - LAGS // 2) % S
+    lag_scale = np.float32(1.0) / np.sqrt(np.float32(F))
+    lags = np.stack([angle_parts(band, shifts, lag_scale).reshape(-1, LAGS) for band in order])
+    return [table.astype(jnp.bfloat16) for table in (forward, backward, lags)]
+
+
+def dot(left, right, left_dim=1, right_dim=0):
+    return lax.dot_general(
+        left,
+        right,
+        (((left_dim,), (right_dim,)), ((), ())),
+        preferred_element_type=jnp.float32,
+    )
+
+
+def fused_kernel(
+    sizes, x, pairs, observed, mask, forward_hbm, backward_hbm, lags_hbm, out,
+    forward, backward, lags, stage1, inbox1, signal, stage2, inbox2, picked, select, stage3, inbox3,
+    inbox4, stage5, inbox5, stage6, inbox6, load_sem,
+    send1, recv1, send2, recv2, send3, recv3, send4, recv4, send5, recv5, send6, recv6,
+):
+    fibres, segs, recs = sizes
+    bands = fibres * segs
+    owners = bands * recs
+    g, f, s, r = (lax.axis_index(name) for name in ("groups", "fibre", "seg", "rec"))
+    band = f * segs + s
+    mine = band * recs + r
+    span, width = x.shape
+    rows = span // 2
+    chans = width // fibres
+    freqs = F // bands
+    low = jnp.bfloat16
+
+    def at(fibre, seg, rec):
+        return (g, fibre, seg, rec)
+
+    def at_band(index):
+        return at(index // segs, index % segs, r)
+
+    def push(src, dst, send, recv, device):
+        copy = pltpu.make_async_remote_copy(
+            src_ref=src, dst_ref=dst, send_sem=send, recv_sem=recv,
+            device_id=device, device_id_type=pl.DeviceIdType.MESH,
+        )
+        copy.start()
+        return copy
+
+    def arrived(dst, recv):
+        pltpu.make_async_remote_copy(
+            src_ref=dst, dst_ref=dst, send_sem=recv, recv_sem=recv,
+            device_id=at(f, s, 1 - r), device_id_type=pl.DeviceIdType.MESH,
+        ).wait_recv()
+
+    sends = []
+    for j in range(fibres):
+        part = x[:, j * chans : (j + 1) * chans]
+        stage1[j] = jnp.concatenate([part[:rows], part[rows:]], axis=1)
+    for d in range(1, fibres):
+        j = (f + d) % fibres
+        sends.append(push(stage1.at[j], inbox1.at[f], send1.at[d - 1], recv1.at[f], at(j, s, r)))
+    loads = [
+        pltpu.make_async_copy(forward_hbm, forward, load_sem.at[0]),
+        pltpu.make_async_copy(lags_hbm.at[band], lags, load_sem.at[1]),
+        pltpu.make_async_copy(backward_hbm, backward, load_sem.at[2]),
+    ]
+    for load in loads:
+        load.start()
+    inbox1[f] = stage1[f]
+
+    total = select.shape[0]
+    count = pairs.shape[0] * BLOCK
+    lane = lax.broadcasted_iota(jnp.int32, (1, 2 * count), 1)
+    target = lane
+    for side in range(2):
+        for n in range(pairs.shape[0]):
+            first = side * count + n * BLOCK
+            inside = (lane >= first) & (lane < first + BLOCK)
+            target = jnp.where(inside, lane + (pairs[n, side] * BLOCK - first), target)
+    row = lax.broadcasted_iota(jnp.int32, (total, 2 * count), 0)
+    select[...] = jnp.where(row == target, 1.0, 0.0).astype(low)
+
+    for d in range(1, fibres):
+        k = (f + d) % fibres
+        arrived(inbox1.at[k], recv1.at[k])
+    for h in range(fibres // 2):
+        early = inbox1[h].astype(jnp.float32)
+        late = inbox1[h + fibres // 2].astype(jnp.float32)
+        for parity, value in enumerate((early + late, early - late)):
+            value = value.astype(low)
+            base = parity * (S // 2) + h * span
+            signal[base : base + rows] = value[:, :chans]
+            signal[base + rows : base + span] = value[:, chans:]
+
+    loads[0].wait()
+    for d in list(range(1, bands)) + [0]:
+        j = (band + d) % bands
+        parity = j // (bands // 2)
+        table = forward[pl.ds(pl.multiple_of(j * 2 * freqs, 2 * freqs), 2 * freqs), :]
+        held = signal[pl.ds(pl.multiple_of(parity * (S // 2), S // 2), S // 2), :]
+        result = dot(table, held).astype(low)
+        packed = jnp.concatenate([result[:freqs], result[freqs:]], axis=1)
+        if d == 0:
+            inbox2[band] = packed
+        else:
+            stage2[d - 1] = packed
+            sends.append(
+                push(stage2.at[d - 1], inbox2.at[band], send2.at[d - 1], recv2.at[band], at_band(j))
+            )
+    for d in range(1, bands):
+        k = (band + d) % bands
+        arrived(inbox2.at[k], recv2.at[k])
+    order = [fibre * segs + seg for seg in range(segs) for fibre in range(fibres)]
+    spectra = jnp.concatenate(
+        [
+            jnp.concatenate([inbox2[k][:, p * chans : (p + 1) * chans] for k in order], axis=1)
+            for p in range(2)
+        ],
+        axis=0,
+    )
+    picked[...] = dot(spectra, select[...])
+    a0, a1 = (picked[:freqs, :count], picked[freqs:, :count])
+    b0, b1 = (picked[:freqs, count:], picked[freqs:, count:])
+    cross = jnp.concatenate([a0 * b0 + a1 * b1, a1 * b0 - a0 * b1], axis=0).astype(low)
+    loads[1].wait()
+    partial = dot(cross, lags[...], 0, 0).astype(low)
+    stage3[...] = partial.reshape(stage3.shape)
+    for d in range(1, owners):
+        j = (mine + d) % owners
+        device = at(j // (segs * recs), j // recs % segs, j % recs)
+        sends.append(push(stage3.at[j], inbox3.at[mine], send3.at[d - 1], recv3.at[mine], device))
+    inbox3[mine] = stage3[mine]
+    for d in range(1, owners):
+        k = (mine + d) % owners
+        arrived(inbox3.at[k], recv3.at[k])
+    synthetic = inbox3[0].astype(jnp.float32)
+    for k in range(1, owners):
+        synthetic += inbox3[k].astype(jnp.float32)
+    window = mask[pl.ds(r, 1), :].astype(jnp.float32)
+    inbox4[mine] = (window * jnp.tanh(synthetic - observed[r])).astype(low)
+    for d in range(1, owners):
+        j = (mine + d) % owners
+        device = at(j // (segs * recs), j // recs % segs, j % recs)
+        sends.append(push(inbox4.at[mine], inbox4.at[mine], send4.at[d - 1], recv4.at[mine], device))
+    for d in range(1, owners):
+        k = (mine + d) % owners
+        arrived(inbox4.at[k], recv4.at[k])
+    weights = inbox4[...].reshape(count, LAGS)
+    adjoint = dot(lags[...], weights, 1, 1).astype(low).astype(jnp.float32)
+    g0, g1 = (adjoint[:freqs], adjoint[freqs:])
+    a0, a1 = (picked[:freqs, :count], picked[freqs:, :count])
+    b0, b1 = (picked[:freqs, count:], picked[freqs:, count:])
+    grads = jnp.concatenate(
+        [
+            jnp.concatenate([g0 * b0 - g1 * b1, g0 * a0 + g1 * a1], axis=1),
+            jnp.concatenate([g0 * b1 + g1 * b0, g0 * a1 - g1 * a0], axis=1),
+        ],
+        axis=0,
+    ).astype(low)
+    summed = dot(grads, select[...], 1, 1).astype(low)
+    for place, k in enumerate(order):
+        cut = slice(place * chans, (place + 1) * chans)
+        stage5[k] = jnp.concatenate([summed[:freqs, cut], summed[freqs:, cut]], axis=1)
+    for d in range(1, bands):
+        j = (band + d) % bands
+        sends.append(push(stage5.at[j], inbox5.at[band], send5.at[d - 1], recv5.at[band], at_band(j)))
+    inbox5[band] = stage5[band]
+    loads[2].wait()
+    for d in range(1, bands):
+        k = (band + d) % bands
+        arrived(inbox5.at[k], recv5.at[k])
+    held = []
+    for parity in range(2):
+        pieces = []
+        for k in range(parity * bands // 2, (parity + 1) * bands // 2):
+            pieces += [inbox5[k][:, :chans], inbox5[k][:, chans:]]
+        held.append(jnp.concatenate(pieces, axis=0))
+    for h in range(fibres // 2):
+        cut = slice(h * span, (h + 1) * span)
+        even = dot(backward[0, cut], held[0])
+        odd = dot(backward[1, cut], held[1])
+        for late, value in enumerate((even + odd, even - odd)):
+            value = value.astype(low)
+            stage6[h + late * (fibres // 2)] = jnp.concatenate([value[:rows], value[rows:]], axis=1)
+    for d in range(1, fibres):
+        j = (f + d) % fibres
+        sends.append(push(stage6.at[j], inbox6.at[f], send6.at[d - 1], recv6.at[f], at(j, s, r)))
+    inbox6[f] = stage6[f]
+    for d in range(1, fibres):
+        k = (f + d) % fibres
+        arrived(inbox6.at[k], recv6.at[k])
+    out[:rows, :] = jnp.concatenate([inbox6[k][:, :chans] for k in range(fibres)], axis=1)
+    out[rows:, :] = jnp.concatenate([inbox6[k][:, chans:] for k in range(fibres)], axis=1)
+    for copy in sends:
+        copy.wait_send()
+
+
+def fused_on_device(mesh_shape, tables, records, pairs, observed, lag_mask):
+    fibres, segs, recs = (mesh_shape[name] for name in ("fibre", "seg", "rec"))
+    bands = fibres * segs
+    owners = bands * recs
+    _, span, width = records.shape
+    freqs = F // bands
+    chans = width // fibres
+    count = pairs.shape[0] * BLOCK
+    low = jnp.bfloat16
+    vmem = pl.BlockSpec(memory_space=pltpu.VMEM)
+    hbm = pl.BlockSpec(memory_space=pltpu.HBM)
+    row = (freqs, 2 * chans)
+    slab = (span // 2, 2 * chans)
+    corr = (BLOCK, LAGS)
+
+    def sems(size):
+        return [pltpu.SemaphoreType.DMA((size - 1,)), pltpu.SemaphoreType.DMA((size,))]
+
+    result = pl.pallas_call(
+        functools.partial(fused_kernel, (fibres, segs, recs)),
+        out_shape=jax.ShapeDtypeStruct((span, width), low),
+        in_specs=[vmem, pl.BlockSpec(memory_space=pltpu.SMEM), vmem, vmem, hbm, hbm, hbm],
+        out_specs=vmem,
+        scratch_shapes=[
+            pltpu.VMEM((2 * F, S // 2), low),
+            pltpu.VMEM((2, S // 2, F), low),
+            pltpu.VMEM((2 * freqs, LAGS), low),
+            pltpu.VMEM((fibres,) + slab, low),
+            pltpu.VMEM((fibres,) + slab, low),
+            pltpu.VMEM((S, chans), low),
+            pltpu.VMEM((bands - 1,) + row, low),
+            pltpu.VMEM((bands,) + row, low),
+            pltpu.VMEM((2 * freqs, 2 * count), jnp.float32),
+            pltpu.VMEM((segs * width, 2 * count), low),
+            pltpu.VMEM((owners,) + corr, low),
+            pltpu.VMEM((owners,) + corr, low),
+            pltpu.VMEM((owners,) + corr, low),
+            pltpu.VMEM((bands,) + row, low),
+            pltpu.VMEM((bands,) + row, low),
+            pltpu.VMEM((fibres,) + slab, low),
+            pltpu.VMEM((fibres,) + slab, low),
+            pltpu.SemaphoreType.DMA((3,)),
+            *sems(fibres), *sems(bands), *sems(owners), *sems(owners), *sems(bands), *sems(fibres),
+        ],
+        compiler_params=pltpu.CompilerParams(
+            has_side_effects=True, vmem_limit_bytes=40 * 1024 * 1024
+        ),
+        name="adjoint",
+    )(records[0], pairs, observed, lag_mask, *tables)
+    return result[None]
+
+
+def fits_fused(shape, records, pairs):
+    fibres, segs, recs = (shape[name] for name in ("fibre", "seg", "rec"))
+    chans = records.shape[2] // (shape["groups"] * segs * fibres)
+    return (
+        fibres == 4
+        and recs == 2
+        and 2 * chans == 128
+        and pairs.shape[0] == fibres * segs * recs
+        and F // (fibres * segs) >= 16
+    )
+
+
 def solution(mesh):
     in_specs = (
         P("rec", "fibre", ("groups", "seg")),
@@ -137,6 +416,21 @@
         P(("groups", "fibre", "seg"), None),
     )
     out_specs = P("rec", "fibre", ("groups", "seg"))
-    return jax.shard_map(
-        on_device, mesh=mesh, in_specs=in_specs, out_specs=out_specs, check_vma=False
-    )
+    shape = dict(mesh.shape)
+
+    def run(records, pairs, observed, lag_mask):
+        args = (records, pairs, observed, lag_mask)
+        if not fits_fused(shape, records, pairs):
+            return jax.shard_map(
+                on_device, mesh=mesh, in_specs=in_specs, out_specs=out_specs, check_vma=False
+            )(*args)
+        tables = [jnp.asarray(t) for t in band_tables(shape["fibre"] * shape["seg"])]
+
+        def body(*blocks):
+            return fused_on_device(shape, tables, *blocks)
+
+        return jax.shard_map(
+            body, mesh=mesh, in_specs=in_specs, out_specs=out_specs, check_vma=False
+        )(*args)
+
+    return run

time: 164 us -> 64.8 us (0.40)
  Pallas kernels: 0 us -> 55 us
  other arithmetic: 50.7 us -> 0 us
  local copies, waits for them, and re-layouts: 39.9 us -> 9.53 us
  starting transfers between devices: 23 us -> 0 us
  waiting for transfers between devices: 21.9 us -> 0 us
  blocking collectives: 16.7 us -> 0 us
  matrix products: 10.8 us -> 0 us
    pallas_call x0 -> x1, Pallas kernels: none -> 55 us  [fused_on_device(): pl.pallas_call(functools.partial(fused_kernel, (fibres, segs, recs)), out...]
    convert_element_type x8 -> x0, other arithmetic: 39.8 us -> none  [the longest x1 35 us: forward_table(): (-jnp.sin(angles) * scale).astype(jnp.bfloat16)]
    all_to_all x5 -> x0, starting transfers between devices: 23 us -> none  [the longest x1 6.35 us: on_device(): lax.all_to_all(spans, 'fibre', split_axis=2, concat_axis=1, tiled=True)]
    all_to_all x5 -> x0, waiting for transfers between devices: 21.9 us -> none  [the longest x1 9.42 us: on_device(): lax.all_to_all(adjoint_spec, ('fibre', 'seg'), split_axis=0, concat_axis=...]
    another operation x1 -> x0, local copies, waits for them, and re-layouts: 16.4 us -> none  [forward_table(): jnp.stack([(jnp.cos(angles) * scale).astype(jnp.bfloat16), (-jnp.sin(angl...]
    reshape x5 -> x0, local copies, waits for them, and re-layouts: 14.5 us -> none  [the longest x1 13.1 us: synthesize(): table.reshape(2 * F, S)]
    all_to_all x1 -> x0, blocking collectives: 13.3 us -> none  [on_device(): lax.all_to_all(sources, 'fibre', split_axis=0, concat_axis=1, tiled=True)]
    dot_general x4 -> x0, matrix products: 10.8 us -> none  [the longest x1 5.06 us: on_device(): jnp.einsum('qs,sn->qn', table.reshape(2 * F, S), signal, preferred_elemen...]
  transfers between devices with their start and end apart: 5 -> 0, of which waited for: 3 -> 0; matrix products, arithmetic and copies ran while one was open for 47% -> 0% of each run, Pallas kernels for 0% -> 0%
where the time goes in v1:
time: 64.8 us; the launch traced here: 64.5 us
  Pallas kernels  55 us (85%)
  local copies, waits for them, and re-layouts  9.53 us (15%)
    pallas_call x1, Pallas kernels, fused_on_device(): pl.pallas_call(functools.partial(fused_kernel, (fibres, segs, recs)), out...  55 us
    unnamed x14, local copies, waits for them, and re-layouts  9.53 us

profile of v1, /device:TPU:0, one launch (start us, length us, event | category | flops | bytes accessed | tf_op | source)
XLA Modules:
  0.0 64.5 jit_solution(884955920032587488)
XLA Ops:
  0.0 0.8 %copy.8.pairs = s32[16,2]{1,0:T(8,128)S(1)} copy(s32[16,2]{0,1:T(2,128)} %param.8) | data formatting | bytes 256 | tf_op args[1]
  0.8 0.0 copy-start
  0.8 2.2 %copy-done = bf16[2,1024,1024]{2,1,0:T(8,128)(2,1)S(1)} copy-done((bf16[2,1024,1024]{2,1,0:T(8,128)(2,1)S(1)}, bf16[2,1024,1024]{2,1,0:T(8,128)(2,1)}, u32[]{:S(2)}) %copy-start) | copy-done | bytes 4194328
  2.9 0.0 copy-start.1
  2.9 2.2 %copy-done.1 = bf16[2048,1024]{1,0:T(8,128)(2,1)S(1)} copy-done((bf16[2048,1024]{1,0:T(8,128)(2,1)S(1)}, bf16[2048,1024]{1,0:T(8,128)(2,1)}, u32[]{:S(2)}) %copy-start.1) | copy-done | bytes 4194328
  5.1 0.0 copy-start.2
  5.1 1.2 %copy-done.2 = bf16[8,256,256]{2,1,0:T(8,128)(2,1)S(1)} copy-done((bf16[8,256,256]{2,1,0:T(8,128)(2,1)S(1)}, bf16[8,256,256]{2,1,0:T(8,128)(2,1)}, u32[]{:S(2)}) %copy-start.2) | copy-done | bytes 1048600
  6.4 0.0 copy-start.3
  6.4 0.9 %copy-done.3 = bf16[1,512,256]{2,1,0:T(8,128)(2,1)S(1)} copy-done((bf16[1,512,256]{2,1,0:T(8,128)(2,1)S(1)}, bf16[1,512,256]{2,1,0:T(8,128)(2,1)}, u32[]{:S(2)}) %copy-start.3) | copy-done | bytes 262168
  7.3 0.0 copy-start.4
  7.3 0.8 %copy-done.4 = f32[2,32,256]{2,1,0:T(8,128)S(1)} copy-done((f32[2,32,256]{2,1,0:T(8,128)S(1)}, f32[2,32,256]{2,1,0:T(8,128)}, u32[]{:S(2)}) %copy-start.4) | copy-done | bytes 65560
  8.1 0.0 copy-start.5
  8.2 0.7 %copy-done.5 = s32[2,256]{1,0:T(2,128)S(1)} copy-done((s32[2,256]{1,0:T(2,128)S(1)}, s32[2,256]{1,0:T(2,128)}, u32[]{:S(2)}) %copy-start.5) | copy-done | bytes 2072
  8.8 55.0 %adjoint.1 = bf16[512,256]{1,0:T(8,128)(2,1)S(1)} custom-call(bf16[512,256]{1,0:T(8,128)(2,1)S(1)} %bitcast.3, s32[16,2]{1,0:T(8,128)S(1)} %copy.8.pairs, f32[2,32,256]{2,1,0:T(8,128)S(1)} %copy-done.4, s32[2,256]{1,0:T(2,128)S(1)} %copy-done.5, bf16[2048,1024]{1,0:T(8,128)(2,1)S(1)} %copy-done.1, bf16[2,1024,1024]{2,1,0:T(8,128)(2,1)S(1)} %copy-done, ...), custom_call_target="tpu_custom_call" | custom-call | tf_op jit(solution)/shard_map/adjoint/pallas_call | solution.py:365
  63.8 0.7 %copy.10 = bf16[1,512,256]{2,1,0:T(8,128)(2,1)} copy(bf16[1,512,256]{2,1,0:T(8,128)(2,1)S(1)} %bitcast.2) | data formatting | bytes 524288
Async XLA Ops:
  0.8 2.2 %copy-start = (bf16[2,1024,1024]{2,1,0:T(8,128)(2,1)S(1)}, bf16[2,1024,1024]{2,1,0:T(8,128)(2,1)}, u32[]{:S(2)}) copy-start(bf16[2,1024,1024]{2,1,0:T(8,128)(2,1)} %constant.7.clone.backward_hbm) | copy-start | bytes 12582916
  2.9 2.2 %copy-start.1 = (bf16[2048,1024]{1,0:T(8,128)(2,1)S(1)}, bf16[2048,1024]{1,0:T(8,128)(2,1)}, u32[]{:S(2)}) copy-start(bf16[2048,1024]{1,0:T(8,128)(2,1)} %constant.6.clone.forward_hbm) | copy-start | bytes 12582916
  5.1 1.2 %copy-start.2 = (bf16[8,256,256]{2,1,0:T(8,128)(2,1)S(1)}, bf16[8,256,256]{2,1,0:T(8,128)(2,1)}, u32[]{:S(2)}) copy-start(bf16[8,256,256]{2,1,0:T(8,128)(2,1)} %constant.8.clone.lags_hbm) | copy-start | bytes 3145732
  6.4 0.9 %copy-start.3 = (bf16[1,512,256]{2,1,0:T(8,128)(2,1)S(1)}, bf16[1,512,256]{2,1,0:T(8,128)(2,1)}, u32[]{:S(2)}) copy-start(bf16[1,512,256]{2,1,0:T(8,128)(2,1)} %param.7) | copy-start | bytes 786436
  7.3 0.8 %copy-start.4 = (f32[2,32,256]{2,1,0:T(8,128)S(1)}, f32[2,32,256]{2,1,0:T(8,128)}, u32[]{:S(2)}) copy-start(f32[2,32,256]{2,1,0:T(8,128)} %observed.1) | copy-start | bytes 196612
  8.1 0.7 %copy-start.5 = (s32[2,256]{1,0:T(2,128)S(1)}, s32[2,256]{1,0:T(2,128)}, u32[]{:S(2)}) copy-start(s32[2,256]{1,0:T(2,128)} %mask.1) | copy-start | bytes 6148

commit v2 on v1

--- a/solution.py
+++ b/solution.py
@@ -13,6 +13,7 @@
 LAGS = 256
 BLOCK = 32
 CH_DEV = 64
+VMEM_GRANT = 67_043_328
 
 
 def forward_table():
@@ -164,8 +165,8 @@
 
 
 def fused_kernel(
-    sizes, x, pairs, observed, mask, forward_hbm, backward_hbm, lags_hbm, out,
-    forward, backward, lags, stage1, inbox1, signal, stage2, inbox2, picked, select, stage3, inbox3,
+    sizes, x_hbm, pairs, observed_hbm, mask_hbm, forward_hbm, backward_hbm, lags_hbm, out,
+    x, observed, mask, forward, backward, lags, stage1, inbox1, signal, stage2, inbox2, picked, select, stage3, inbox3,
     inbox4, stage5, inbox5, stage6, inbox6, load_sem,
     send1, recv1, send2, recv2, send3, recv3, send4, recv4, send5, recv5, send6, recv6,
 ):
@@ -202,30 +203,35 @@
         ).wait_recv()
 
     sends = []
+    first_load = pltpu.make_async_copy(x_hbm, x, load_sem.at[0])
+    first_load.start()
+    loads = [
+        pltpu.make_async_copy(forward_hbm, forward, load_sem.at[1]),
+        pltpu.make_async_copy(lags_hbm.at[band], lags, load_sem.at[2]),
+        pltpu.make_async_copy(observed_hbm.at[r], observed, load_sem.at[3]),
+        pltpu.make_async_copy(mask_hbm, mask, load_sem.at[4]),
+        pltpu.make_async_copy(backward_hbm, backward, load_sem.at[5]),
+    ]
+    first_load.wait()
+    for load in loads:
+        load.start()
     for j in range(fibres):
         part = x[:, j * chans : (j + 1) * chans]
         stage1[j] = jnp.concatenate([part[:rows], part[rows:]], axis=1)
     for d in range(1, fibres):
         j = (f + d) % fibres
         sends.append(push(stage1.at[j], inbox1.at[f], send1.at[d - 1], recv1.at[f], at(j, s, r)))
-    loads = [
-        pltpu.make_async_copy(forward_hbm, forward, load_sem.at[0]),
-        pltpu.make_async_copy(lags_hbm.at[band], lags, load_sem.at[1]),
-        pltpu.make_async_copy(backward_hbm, backward, load_sem.at[2]),
-    ]
-    for load in loads:
-        load.start()
     inbox1[f] = stage1[f]
 
     total = select.shape[0]
-    count = pairs.shape[0] * BLOCK
+    count = pairs.shape[1] * BLOCK
     lane = lax.broadcasted_iota(jnp.int32, (1, 2 * count), 1)
     target = lane
     for side in range(2):
-        for n in range(pairs.shape[0]):
+        for n in range(pairs.shape[1]):
             first = side * count + n * BLOCK
             inside = (lane >= first) & (lane < first + BLOCK)
-            target = jnp.where(inside, lane + (pairs[n, side] * BLOCK - first), target)
+            target = jnp.where(inside, lane + (pairs[side, n] * BLOCK - first), target)
     row = lax.broadcasted_iota(jnp.int32, (total, 2 * count), 0)
     select[...] = jnp.where(row == target, 1.0, 0.0).astype(low)
 
@@ -282,11 +288,13 @@
     for d in range(1, owners):
         k = (mine + d) % owners
         arrived(inbox3.at[k], recv3.at[k])
+    loads[2].wait()
+    loads[3].wait()
     synthetic = inbox3[0].astype(jnp.float32)
     for k in range(1, owners):
         synthetic += inbox3[k].astype(jnp.float32)
     window = mask[pl.ds(r, 1), :].astype(jnp.float32)
-    inbox4[mine] = (window * jnp.tanh(synthetic - observed[r])).astype(low)
+    inbox4[mine] = (window * jnp.tanh(synthetic - observed[...])).astype(low)
     for d in range(1, owners):
         j = (mine + d) % owners
         device = at(j // (segs * recs), j // recs % segs, j % recs)
@@ -314,7 +322,7 @@
         j = (band + d) % bands
         sends.append(push(stage5.at[j], inbox5.at[band], send5.at[d - 1], recv5.at[band], at_band(j)))
     inbox5[band] = stage5[band]
-    loads[2].wait()
+    loads[4].wait()
     for d in range(1, bands):
         k = (band + d) % bands
         arrived(inbox5.at[k], recv5.at[k])
@@ -365,9 +373,12 @@
     result = pl.pallas_call(
         functools.partial(fused_kernel, (fibres, segs, recs)),
         out_shape=jax.ShapeDtypeStruct((span, width), low),
-        in_specs=[vmem, pl.BlockSpec(memory_space=pltpu.SMEM), vmem, vmem, hbm, hbm, hbm],
+        in_specs=[hbm, pl.BlockSpec(memory_space=pltpu.SMEM)] + [hbm] * 5,
         out_specs=vmem,
         scratch_shapes=[
+            pltpu.VMEM((span, width), low),
+            pltpu.VMEM(corr, jnp.float32),
+            pltpu.VMEM(lag_mask.shape, jnp.int32),
             pltpu.VMEM((2 * F, S // 2), low),
             pltpu.VMEM((2, S // 2, F), low),
             pltpu.VMEM((2 * freqs, LAGS), low),
@@ -385,14 +396,14 @@
             pltpu.VMEM((bands,) + row, low),
             pltpu.VMEM((fibres,) + slab, low),
             pltpu.VMEM((fibres,) + slab, low),
-            pltpu.SemaphoreType.DMA((3,)),
+            pltpu.SemaphoreType.DMA((6,)),
             *sems(fibres), *sems(bands), *sems(owners), *sems(owners), *sems(bands), *sems(fibres),
         ],
         compiler_params=pltpu.CompilerParams(
-            has_side_effects=True, vmem_limit_bytes=40 * 1024 * 1024
+            has_side_effects=True, vmem_limit_bytes=VMEM_GRANT
         ),
         name="adjoint",
-    )(records[0], pairs, observed, lag_mask, *tables)
+    )(records[0], pairs.T, observed, lag_mask, *tables)
     return result[None]
 
 

time: 64.8 us -> 58.5 us (0.903)
  local copies, waits for them, and re-layouts: 9.53 us -> 1.67 us
  Pallas kernels: 55 us -> 56.7 us
    unnamed x14 -> x1, local copies, waits for them, and re-layouts: 9.53 us -> 1.67 us
    pallas_call x1, Pallas kernels: 55 us -> 56.7 us  [fused_on_device(): pl.pallas_call(functools.partial(fused_kernel, (fibres, segs, recs)), out...]
where the time goes in v2:
time: 58.5 us; the launch traced here: 58.4 us
  Pallas kernels  56.7 us (97%)
  local copies, waits for them, and re-layouts  1.67 us (3%)
    pallas_call x1, Pallas kernels, fused_on_device(): pl.pallas_call(functools.partial(fused_kernel, (fibres, segs, recs)), out...  56.7 us
    unnamed x1, local copies, waits for them, and re-layouts  1.67 us

profile of v2, /device:TPU:0, one launch (start us, length us, event | category | flops | bytes accessed | tf_op | source)
XLA Modules:
  0.0 58.4 jit_solution(165187829443671248)
XLA Ops:
  0.0 56.7 %adjoint.1 = bf16[512,256]{1,0:T(8,128)(2,1)} custom-call(bf16[512,256]{1,0:T(8,128)(2,1)} %bitcast.4, s32[2,16]{1,0:T(2,128)} %bitcast.5, f32[2,32,256]{2,1,0:T(8,128)} %observed_hbm.1, s32[2,256]{1,0:T(2,128)} %mask_hbm.1, bf16[2048,1024]{1,0:T(8,128)(2,1)} %constant.6.clone.forward_hbm, bf16[2,1024,1024]{2,1,0:T(8,128)(2,1)} %constant.7.clone.backward_hbm, ...), custom_call_target="tpu_custom_call" | custom-call | tf_op jit(solution)/shard_map/adjoint/pallas_call | solution.py:373
  56.7 1.7 %copy.9 = bf16[1,512,256]{2,1,0:T(8,128)(2,1)} copy(bf16[1,512,256]{2,1,0:T(8,128)(2,1)} %bitcast.3) | data formatting | bytes 524288

commit v3 on v2

--- a/solution.py
+++ b/solution.py
@@ -166,16 +166,15 @@
 
 def fused_kernel(
     sizes, x_hbm, pairs, observed_hbm, mask_hbm, forward_hbm, backward_hbm, lags_hbm, out,
-    x, observed, mask, forward, backward, lags, stage1, inbox1, signal, stage2, inbox2, picked, select, stage3, inbox3,
-    inbox4, stage5, inbox5, stage6, inbox6, load_sem,
+    x, observed, mask, forward, backward, lags, stage1, inbox1, signal, stage2, inbox2, picked, select, cross,
+    stage_core, inbox_core, stage3, inbox3, inbox4, stage5, inbox5, stage6, inbox6, load_sem,
+    core_sem, relay_send, relay_recv,
     send1, recv1, send2, recv2, send3, recv3, send4, recv4, send5, recv5, send6, recv6,
 ):
     fibres, segs, recs = sizes
     bands = fibres * segs
-    owners = bands * recs
     g, f, s, r = (lax.axis_index(name) for name in ("groups", "fibre", "seg", "rec"))
     band = f * segs + s
-    mine = band * recs + r
     span, width = x.shape
     rows = span // 2
     chans = width // fibres
@@ -202,6 +201,15 @@
             device_id=at(f, s, 1 - r), device_id_type=pl.DeviceIdType.MESH,
         ).wait_recv()
 
+    def flipped(index, bits):
+        result, bit = 0, 1
+        while bit < bands:
+            digit = index // bit % 2
+            result += bit * (1 - digit if bits // bit % 2 else digit)
+            bit *= 2
+        return result
+
+    partner = at(f, s, 1 - r)
     sends = []
     first_load = pltpu.make_async_copy(x_hbm, x, load_sem.at[0])
     first_load.start()
@@ -218,8 +226,8 @@
     for j in range(fibres):
         part = x[:, j * chans : (j + 1) * chans]
         stage1[j] = jnp.concatenate([part[:rows], part[rows:]], axis=1)
-    for d in range(1, fibres):
-        j = (f + d) % fibres
+    for d in range(fibres - 1, 0, -1):
+        j = flipped(f, d)
         sends.append(push(stage1.at[j], inbox1.at[f], send1.at[d - 1], recv1.at[f], at(j, s, r)))
     inbox1[f] = stage1[f]
 
@@ -230,6 +238,7 @@
     for side in range(2):
         for n in range(pairs.shape[1]):
             first = side * count + n * BLOCK
+            n = n % bands * recs + n // bands
             inside = (lane >= first) & (lane < first + BLOCK)
             target = jnp.where(inside, lane + (pairs[side, n] * BLOCK - first), target)
     row = lax.broadcasted_iota(jnp.int32, (total, 2 * count), 0)
@@ -248,20 +257,21 @@
             signal[base + rows : base + span] = value[:, chans:]
 
     loads[0].wait()
-    for d in list(range(1, bands)) + [0]:
-        j = (band + d) % bands
-        parity = j // (bands // 2)
-        table = forward[pl.ds(pl.multiple_of(j * 2 * freqs, 2 * freqs), 2 * freqs), :]
+    half = bands // 2
+    for far in (1, 0):
+        parity = flipped(f, far * (fibres // 2)) // (fibres // 2)
+        top = pl.multiple_of(parity * F, F)
         held = signal[pl.ds(pl.multiple_of(parity * (S // 2), S // 2), S // 2), :]
-        result = dot(table, held).astype(low)
-        packed = jnp.concatenate([result[:freqs], result[freqs:]], axis=1)
-        if d == 0:
-            inbox2[band] = packed
-        else:
-            stage2[d - 1] = packed
+        result = dot(forward[pl.ds(top, F), :], held).astype(low)
+        for i in range(half):
+            block = result[i * 2 * freqs : (i + 1) * 2 * freqs]
+            stage2[parity * half + i] = jnp.concatenate([block[:freqs], block[freqs:]], axis=1)
+        for d in range((far + 1) * half - 1, max(far * half - 1, 0), -1):
+            j = flipped(band, d)
             sends.append(
-                push(stage2.at[d - 1], inbox2.at[band], send2.at[d - 1], recv2.at[band], at_band(j))
+                push(stage2.at[j], inbox2.at[band], send2.at[d - 1], recv2.at[band], at_band(j))
             )
+    inbox2[band] = stage2[band]
     for d in range(1, bands):
         k = (band + d) % bands
         arrived(inbox2.at[k], recv2.at[k])
@@ -274,34 +284,48 @@
         axis=0,
     )
     picked[...] = dot(spectra, select[...])
-    a0, a1 = (picked[:freqs, :count], picked[freqs:, :count])
-    b0, b1 = (picked[:freqs, count:], picked[freqs:, count:])
-    cross = jnp.concatenate([a0 * b0 + a1 * b1, a1 * b0 - a0 * b1], axis=0).astype(low)
+    share = count // recs
+    for h in range(recs):
+        a0, a1, b0, b1 = (
+            picked[p * freqs : (p + 1) * freqs, side * count + h * share : side * count + (h + 1) * share]
+            for side in range(2)
+            for p in range(2)
+        )
+        cross[h] = jnp.concatenate([a0 * b0 + a1 * b1, a1 * b0 - a0 * b1], axis=0).astype(low)
     loads[1].wait()
-    partial = dot(cross, lags[...], 0, 0).astype(low)
+    stage_core[...] = dot(cross[1 - r], lags[...], 0, 0).astype(low)
+    sends.append(push(stage_core, inbox_core, core_sem.at[0], core_sem.at[1], partner))
+    partial = dot(cross[r], lags[...], 0, 0)
+    arrived(inbox_core, core_sem.at[1])
+    partial = (partial + inbox_core[...].astype(jnp.float32)).astype(low)
     stage3[...] = partial.reshape(stage3.shape)
-    for d in range(1, owners):
-        j = (mine + d) % owners
-        device = at(j // (segs * recs), j // recs % segs, j % recs)
-        sends.append(push(stage3.at[j], inbox3.at[mine], send3.at[d - 1], recv3.at[mine], device))
-    inbox3[mine] = stage3[mine]
-    for d in range(1, owners):
-        k = (mine + d) % owners
-        arrived(inbox3.at[k], recv3.at[k])
+    for d in range(bands - 1, 0, -1):
+        j = flipped(band, d)
+        sends.append(push(stage3.at[j], inbox3.at[band], send3.at[d - 1], recv3.at[band], at_band(j)))
+    inbox3[band] = stage3[band]
     loads[2].wait()
     loads[3].wait()
+    for d in range(1, bands):
+        k = flipped(band, d)
+        arrived(inbox3.at[k], recv3.at[k])
     synthetic = inbox3[0].astype(jnp.float32)
-    for k in range(1, owners):
+    for k in range(1, bands):
         synthetic += inbox3[k].astype(jnp.float32)
     window = mask[pl.ds(r, 1), :].astype(jnp.float32)
-    inbox4[mine] = (window * jnp.tanh(synthetic - observed[...])).astype(low)
-    for d in range(1, owners):
-        j = (mine + d) % owners
-        device = at(j // (segs * recs), j // recs % segs, j % recs)
-        sends.append(push(inbox4.at[mine], inbox4.at[mine], send4.at[d - 1], recv4.at[mine], device))
-    for d in range(1, owners):
-        k = (mine + d) % owners
-        arrived(inbox4.at[k], recv4.at[k])
+    inbox4[r, band] = (window * jnp.tanh(synthetic - observed[...])).astype(low)
+    own = inbox4.at[r, band]
+    for d in range(bands - 1, 0, -1):
+        j = flipped(band, d)
+        sends.append(push(own, own, send4.at[d - 1], recv4.at[band], at_band(j)))
+    sends.append(push(own, own, relay_send.at[0], relay_recv.at[band], partner))
+    for d in range(1, bands):
+        k = flipped(band, d)
+        arrived(inbox4.at[r, k], recv4.at[k])
+        got = inbox4.at[r, k]
+        sends.append(push(got, got, relay_send.at[d], relay_recv.at[k], partner))
+    for d in range(bands):
+        k = flipped(band, d)
+        arrived(inbox4.at[1 - r, k], relay_recv.at[k])
     weights = inbox4[...].reshape(count, LAGS)
     adjoint = dot(lags[...], weights, 1, 1).astype(low).astype(jnp.float32)
     g0, g1 = (adjoint[:freqs], adjoint[freqs:])
@@ -318,8 +342,8 @@
     for place, k in enumerate(order):
         cut = slice(place * chans, (place + 1) * chans)
         stage5[k] = jnp.concatenate([summed[:freqs, cut], summed[freqs:, cut]], axis=1)
-    for d in range(1, bands):
-        j = (band + d) % bands
+    for d in range(bands - 1, 0, -1):
+        j = flipped(band, d)
         sends.append(push(stage5.at[j], inbox5.at[band], send5.at[d - 1], recv5.at[band], at_band(j)))
     inbox5[band] = stage5[band]
     loads[4].wait()
@@ -332,16 +356,18 @@
         for k in range(parity * bands // 2, (parity + 1) * bands // 2):
             pieces += [inbox5[k][:, :chans], inbox5[k][:, chans:]]
         held.append(jnp.concatenate(pieces, axis=0))
-    for h in range(fibres // 2):
-        cut = slice(h * span, (h + 1) * span)
-        even = dot(backward[0, cut], held[0])
-        odd = dot(backward[1, cut], held[1])
+    for i in range(1, -1, -1):
+        h = flipped(f, i) % 2
+        cut = pl.ds(pl.multiple_of(h * span, span), span)
+        even = dot(backward[0, cut, :], held[0])
+        odd = dot(backward[1, cut, :], held[1])
         for late, value in enumerate((even + odd, even - odd)):
             value = value.astype(low)
-            stage6[h + late * (fibres // 2)] = jnp.concatenate([value[:rows], value[rows:]], axis=1)
-    for d in range(1, fibres):
-        j = (f + d) % fibres
-        sends.append(push(stage6.at[j], inbox6.at[f], send6.at[d - 1], recv6.at[f], at(j, s, r)))
+            stage6[h + late * 2] = jnp.concatenate([value[:rows], value[rows:]], axis=1)
+        for d in (2 + i, i):
+            if d > 0:
+                j = flipped(f, d)
+                sends.append(push(stage6.at[j], inbox6.at[f], send6.at[d - 1], recv6.at[f], at(j, s, r)))
     inbox6[f] = stage6[f]
     for d in range(1, fibres):
         k = (f + d) % fibres
@@ -355,7 +381,6 @@
 def fused_on_device(mesh_shape, tables, records, pairs, observed, lag_mask):
     fibres, segs, recs = (mesh_shape[name] for name in ("fibre", "seg", "rec"))
     bands = fibres * segs
-    owners = bands * recs
     _, span, width = records.shape
     freqs = F // bands
     chans = width // fibres
@@ -385,19 +410,25 @@
             pltpu.VMEM((fibres,) + slab, low),
             pltpu.VMEM((fibres,) + slab, low),
             pltpu.VMEM((S, chans), low),
-            pltpu.VMEM((bands - 1,) + row, low),
+            pltpu.VMEM((bands,) + row, low),
             pltpu.VMEM((bands,) + row, low),
             pltpu.VMEM((2 * freqs, 2 * count), jnp.float32),
             pltpu.VMEM((segs * width, 2 * count), low),
-            pltpu.VMEM((owners,) + corr, low),
-            pltpu.VMEM((owners,) + corr, low),
-            pltpu.VMEM((owners,) + corr, low),
+            pltpu.VMEM((recs, 2 * freqs, count // recs), low),
+            pltpu.VMEM((count // recs, LAGS), low),
+            pltpu.VMEM((count // recs, LAGS), low),
+            pltpu.VMEM((bands,) + corr, low),
+            pltpu.VMEM((bands,) + corr, low),
+            pltpu.VMEM((recs, bands) + corr, low),
             pltpu.VMEM((bands,) + row, low),
             pltpu.VMEM((bands,) + row, low),
             pltpu.VMEM((fibres,) + slab, low),
             pltpu.VMEM((fibres,) + slab, low),
             pltpu.SemaphoreType.DMA((6,)),
-            *sems(fibres), *sems(bands), *sems(owners), *sems(owners), *sems(bands), *sems(fibres),
+            pltpu.SemaphoreType.DMA((2,)),
+            pltpu.SemaphoreType.DMA((bands,)),
+            pltpu.SemaphoreType.DMA((bands,)),
+            *sems(fibres), *sems(bands), *sems(bands), *sems(bands), *sems(bands), *sems(fibres),
         ],
         compiler_params=pltpu.CompilerParams(
             has_side_effects=True, vmem_limit_bytes=VMEM_GRANT
@@ -413,6 +444,7 @@
     return (
         fibres == 4
         and recs == 2
+        and segs & (segs - 1) == 0
         and 2 * chans == 128
         and pairs.shape[0] == fibres * segs * recs
         and F // (fibres * segs) >= 16

time: 58.5 us -> 56.3 us (0.962)
  Pallas kernels: 56.7 us -> 54.4 us
    pallas_call x1, Pallas kernels: 56.7 us -> 54.4 us  [fused_on_device(): pl.pallas_call(functools.partial(fused_kernel, (fibres, segs, recs)), out...]
where the time goes in v3:
time: 56.3 us; the launch traced here: 56.1 us
  Pallas kernels  54.4 us (97%)
  local copies, waits for them, and re-layouts  1.67 us (3%)
    pallas_call x1, Pallas kernels, fused_on_device(): pl.pallas_call(functools.partial(fused_kernel, (fibres, segs, recs)), out...  54.4 us
    unnamed x1, local copies, waits for them, and re-layouts  1.67 us

profile of v3, /device:TPU:0, one launch (start us, length us, event | category | flops | bytes accessed | tf_op | source)
XLA Modules:
  0.0 56.1 jit_solution(8552839212650152235)
XLA Ops:
  0.0 54.4 %adjoint.1 = bf16[512,256]{1,0:T(8,128)(2,1)} custom-call(bf16[512,256]{1,0:T(8,128)(2,1)} %bitcast.4, s32[2,16]{1,0:T(2,128)} %bitcast.5, f32[2,32,256]{2,1,0:T(8,128)} %observed_hbm.1, s32[2,256]{1,0:T(2,128)} %mask_hbm.1, bf16[2048,1024]{1,0:T(8,128)(2,1)} %constant.6.clone.forward_hbm, bf16[2,1024,1024]{2,1,0:T(8,128)(2,1)} %constant.7.clone.backward_hbm, ...), custom_call_target="tpu_custom_call" | custom-call | tf_op jit(solution)/shard_map/adjoint/pallas_call | solution.py:398
  54.4 1.7 %copy.9 = bf16[1,512,256]{2,1,0:T(8,128)(2,1)} copy(bf16[1,512,256]{2,1,0:T(8,128)(2,1)} %bitcast.3) | data formatting | bytes 524288

commit v4 on v3

--- a/solution.py
+++ b/solution.py
@@ -13,7 +13,7 @@
 LAGS = 256
 BLOCK = 32
 CH_DEV = 64
-VMEM_GRANT = 67_043_328
+VMEM_GRANT = 66387968
 
 
 def forward_table():
@@ -210,6 +210,12 @@
         return result
 
     partner = at(f, s, 1 - r)
+    barrier = pltpu.get_barrier_semaphore()
+    for d in range(1, bands):
+        pl.semaphore_signal(
+            barrier, inc=1, device_id=at_band(flipped(band, d)), device_id_type=pl.DeviceIdType.MESH
+        )
+    pl.semaphore_signal(barrier, inc=1, device_id=partner, device_id_type=pl.DeviceIdType.MESH)
     sends = []
     first_load = pltpu.make_async_copy(x_hbm, x, load_sem.at[0])
     first_load.start()
@@ -226,6 +232,7 @@
     for j in range(fibres):
         part = x[:, j * chans : (j + 1) * chans]
         stage1[j] = jnp.concatenate([part[:rows], part[rows:]], axis=1)
+    pl.semaphore_wait(barrier, bands)
     for d in range(fibres - 1, 0, -1):
         j = flipped(f, d)
         sends.append(push(stage1.at[j], inbox1.at[f], send1.at[d - 1], recv1.at[f], at(j, s, r)))
@@ -262,15 +269,21 @@
         parity = flipped(f, far * (fibres // 2)) // (fibres // 2)
         top = pl.multiple_of(parity * F, F)
         held = signal[pl.ds(pl.multiple_of(parity * (S // 2), S // 2), S // 2), :]
-        result = dot(forward[pl.ds(top, F), :], held).astype(low)
-        for i in range(half):
-            block = result[i * 2 * freqs : (i + 1) * 2 * freqs]
-            stage2[parity * half + i] = jnp.concatenate([block[:freqs], block[freqs:]], axis=1)
-        for d in range((far + 1) * half - 1, max(far * half - 1, 0), -1):
-            j = flipped(band, d)
-            sends.append(
-                push(stage2.at[j], inbox2.at[band], send2.at[d - 1], recv2.at[band], at_band(j))
-            )
+        for pair in (1, 0):
+            inner = flipped(f % 2, pair)
+            start = pl.multiple_of(top + inner * (F // 2), F // 2)
+            result = dot(forward[pl.ds(start, F // 2), :], held).astype(low)
+            for i in range(segs):
+                block = result[i * 2 * freqs : (i + 1) * 2 * freqs]
+                stage2[parity * half + inner * segs + i] = jnp.concatenate(
+                    [block[:freqs], block[freqs:]], axis=1
+                )
+            first = far * half + pair * segs
+            for d in range(first + segs - 1, max(first - 1, 0), -1):
+                j = flipped(band, d)
+                sends.append(
+                    push(stage2.at[j], inbox2.at[band], send2.at[d - 1], recv2.at[band], at_band(j))
+                )
     inbox2[band] = stage2[band]
     for d in range(1, bands):
         k = (band + d) % bands
@@ -431,7 +444,7 @@
             *sems(fibres), *sems(bands), *sems(bands), *sems(bands), *sems(bands), *sems(fibres),
         ],
         compiler_params=pltpu.CompilerParams(
-            has_side_effects=True, vmem_limit_bytes=VMEM_GRANT
+            has_side_effects=True, collective_id=0, vmem_limit_bytes=VMEM_GRANT
         ),
         name="adjoint",
     )(records[0], pairs.T, observed, lag_mask, *tables)

time: 56.3 us -> 52.1 us (0.925)
  Pallas kernels: 54.4 us -> 50.2 us
    pallas_call x1, Pallas kernels: 54.4 us -> 50.2 us  [fused_on_device(): pl.pallas_call(functools.partial(fused_kernel, (fibres, segs, recs)), out...]
where the time goes in v4:
time: 52.1 us; the launch traced here: 51.9 us
  Pallas kernels  50.2 us (96%)
  local copies, waits for them, and re-layouts  1.67 us (3%)
    pallas_call x1, Pallas kernels, fused_on_device(): pl.pallas_call(functools.partial(fused_kernel, (fibres, segs, recs)), out...  50.2 us
    unnamed x1, local copies, waits for them, and re-layouts  1.67 us

profile of v4, /device:TPU:0, one launch (start us, length us, event | category | flops | bytes accessed | tf_op | source)
XLA Modules:
  0.0 51.9 jit_solution(11564461092886615298)
XLA Ops:
  0.0 50.2 %adjoint.1 = bf16[512,256]{1,0:T(8,128)(2,1)} custom-call(bf16[512,256]{1,0:T(8,128)(2,1)} %bitcast.4, s32[2,16]{1,0:T(2,128)} %bitcast.5, f32[2,32,256]{2,1,0:T(8,128)} %observed_hbm.1, s32[2,256]{1,0:T(2,128)} %mask_hbm.1, bf16[2048,1024]{1,0:T(8,128)(2,1)} %constant.6.clone.forward_hbm, bf16[2,1024,1024]{2,1,0:T(8,128)(2,1)} %constant.7.clone.backward_hbm, ...), custom_call_target="tpu_custom_call" | custom-call | tf_op jit(solution)/shard_map/adjoint/pallas_call | solution.py:411
  50.2 1.7 %copy.9 = bf16[1,512,256]{2,1,0:T(8,128)(2,1)} copy(bf16[1,512,256]{2,1,0:T(8,128)(2,1)} %bitcast.3) | data formatting | bytes 524288

commit v5 on v4

--- a/solution.py
+++ b/solution.py
@@ -13,7 +13,7 @@
 LAGS = 256
 BLOCK = 32
 CH_DEV = 64
-VMEM_GRANT = 66387968
+VMEM_GRANT = 60899328
 
 
 def forward_table():
@@ -410,7 +410,7 @@
 
     result = pl.pallas_call(
         functools.partial(fused_kernel, (fibres, segs, recs)),
-        out_shape=jax.ShapeDtypeStruct((span, width), low),
+        out_shape=pltpu.VMEM((span, width), low),
         in_specs=[hbm, pl.BlockSpec(memory_space=pltpu.SMEM)] + [hbm] * 5,
         out_specs=vmem,
         scratch_shapes=[

time: 52.1 us -> 50.4 us (0.967)
  local copies, waits for them, and re-layouts: 1.67 us -> 0.71 us
  Pallas kernels: 50.2 us -> 49.5 us
    unnamed x1, local copies, waits for them, and re-layouts: 1.67 us -> 0.71 us
    pallas_call x1, Pallas kernels: 50.2 us -> 49.5 us  [fused_on_device(): pl.pallas_call(functools.partial(fused_kernel, (fibres, segs, recs)), out...]
where the time goes in v5:
time: 50.4 us; the launch traced here: 50.3 us
  Pallas kernels  49.5 us (98%)
  local copies, waits for them, and re-layouts  0.71 us (1%)
    pallas_call x1, Pallas kernels, fused_on_device(): pl.pallas_call(functools.partial(fused_kernel, (fibres, segs, recs)), out...  49.5 us

profile of v5, /device:TPU:0, one launch (start us, length us, event | category | flops | bytes accessed | tf_op | source)
XLA Modules:
  0.0 50.3 jit_solution(14506531878814779484)
XLA Ops:
  0.0 49.5 %adjoint.1 = bf16[512,256]{1,0:T(8,128)(2,1)S(1)} custom-call(bf16[512,256]{1,0:T(8,128)(2,1)} %bitcast.4, s32[2,16]{1,0:T(2,128)} %bitcast.5, f32[2,32,256]{2,1,0:T(8,128)} %observed_hbm.1, s32[2,256]{1,0:T(2,128)} %mask_hbm.1, bf16[2048,1024]{1,0:T(8,128)(2,1)} %constant.6.clone.forward_hbm, bf16[2,1024,1024]{2,1,0:T(8,128)(2,1)} %constant.7.clone.backward_hbm, ...), custom_call_target="tpu_custom_call" | custom-call | tf_op jit(solution)/shard_map/adjoint/pallas_call | solution.py:411
  49.5 0.7 %copy.9 = bf16[1,512,256]{2,1,0:T(8,128)(2,1)} copy(bf16[1,512,256]{2,1,0:T(8,128)(2,1)S(1)} %bitcast.3) | data formatting | bytes 524288

commit v6 on v5

--- a/solution.py
+++ b/solution.py
@@ -351,13 +351,21 @@
         ],
         axis=0,
     ).astype(low)
-    summed = dot(grads, select[...], 1, 1).astype(low)
-    for place, k in enumerate(order):
-        cut = slice(place * chans, (place + 1) * chans)
-        stage5[k] = jnp.concatenate([summed[:freqs, cut], summed[freqs:, cut]], axis=1)
-    for d in range(bands - 1, 0, -1):
-        j = flipped(band, d)
-        sends.append(push(stage5.at[j], inbox5.at[band], send5.at[d - 1], recv5.at[band], at_band(j)))
+    for far in (1, 0):
+        side = flipped(f, far * (fibres // 2)) // (fibres // 2)
+        for seg in range(segs):
+            start = pl.multiple_of(seg * width + side * (width // 2), width // 2)
+            summed = dot(grads, select[pl.ds(start, width // 2), :], 1, 1).astype(low)
+            for i in range(fibres // 2):
+                cut = slice(i * chans, (i + 1) * chans)
+                stage5[(side * (fibres // 2) + i) * segs + seg] = jnp.concatenate(
+                    [summed[:freqs, cut], summed[freqs:, cut]], axis=1
+                )
+        for d in range((far + 1) * half - 1, max(far * half - 1, 0), -1):
+            j = flipped(band, d)
+            sends.append(
+                push(stage5.at[j], inbox5.at[band], send5.at[d - 1], recv5.at[band], at_band(j))
+            )
     inbox5[band] = stage5[band]
     loads[4].wait()
     for d in range(1, bands):

time: 50.4 us -> 50.5 us (level)
  no operation moved by 1% of the time
where the time goes in v6:
time: 50.5 us; the launch traced here: 50.3 us
  Pallas kernels  49.6 us (98%)
  local copies, waits for them, and re-layouts  0.71 us (1%)
    pallas_call x1, Pallas kernels, fused_on_device(): pl.pallas_call(functools.partial(fused_kernel, (fibres, segs, recs)), out...  49.6 us

profile of v6, /device:TPU:0, one launch (start us, length us, event | category | flops | bytes accessed | tf_op | source)
XLA Modules:
  0.0 50.3 jit_solution(14024594971429068089)
XLA Ops:
  0.0 49.6 %adjoint.1 = bf16[512,256]{1,0:T(8,128)(2,1)S(1)} custom-call(bf16[512,256]{1,0:T(8,128)(2,1)} %bitcast.4, s32[2,16]{1,0:T(2,128)} %bitcast.5, f32[2,32,256]{2,1,0:T(8,128)} %observed_hbm.1, s32[2,256]{1,0:T(2,128)} %mask_hbm.1, bf16[2048,1024]{1,0:T(8,128)(2,1)} %constant.6.clone.forward_hbm, bf16[2,1024,1024]{2,1,0:T(8,128)(2,1)} %constant.7.clone.backward_hbm, ...), custom_call_target="tpu_custom_call" | custom-call | tf_op jit(solution)/shard_map/adjoint/pallas_call | solution.py:419
  49.6 0.7 %copy.9 = bf16[1,512,256]{2,1,0:T(8,128)(2,1)} copy(bf16[1,512,256]{2,1,0:T(8,128)(2,1)S(1)} %bitcast.3) | data formatting | bytes 524288
